TPU v7x, 32 devices: a whole 2x2x4 slice. The times are simulated.
32 devices in a mesh: lat: 4 (over y, x), lon: 8 (over z, core).
Axes of the slice: x: 2, y: 2, z: 4, core: 2. Of those that a mesh axis runs over, the one named last changes fastest.
Arguments:
- activations: bfloat16 [4, 16, 720, 512], P(None, 'lat', 'lon'), may hold values from -48 to 48
- upstream: bfloat16 [4, 16, 720, 512], P(None, 'lat', 'lon'), may hold values from -6 to 6
- master: float32 [512, 9, 512], P(('lat', 'lon')), may hold values from -0.09375 to 0.09375
- moment_one: float32 [512, 9, 512], P(('lat', 'lon')), may hold values from -2.5 to 2.5
- moment_two: float32 [512, 9, 512], P(('lat', 'lon')), may hold values from 0.01 to 1
Outputs:
- input_grad: bfloat16 [4, 16, 720, 512], P(None, 'lat', 'lon')
- new_weights: bfloat16 [512, 9, 512], replicated
- new_master: float32 [512, 9, 512], P(('lat', 'lon'))
- new_moment_one: float32 [512, 9, 512], P(('lat', 'lon'))
- new_moment_two: float32 [512, 9, 512], P(('lat', 'lon'))
- clipped_grad: float32 [512, 9, 512], P(('lat', 'lon'))
All inputs are finite; a program needn't handle non-finite values.
Results may differ from a plain program's by a relative error of at most 0.0049.
Values may be sent and summed in bfloat16 or wider, within the bound.
A program may use at most 128 MiB of HBM per device.

v0:
```python
import math
import jax
import jax.numpy as jnp
from jax import lax
from jax.sharding import PartitionSpec as P

CIN = 512
COUT = 512
TAPS = 9
learn_rate = 0.01
beta_one = 0.9
beta_two = 0.999
adam_eps = 1e-08
decay_rate = 0.1
step_count = 10.0
norm_eps = 1e-06


def padded(block, sides, width):
    for axis, dim in sides:
        count = lax.axis_size(axis)
        forward = [(i, i + 1) for i in range(count - 1)]
        forward.append((count - 1, 0))
        backward = [(target, source) for source, target in forward]
        low = lax.ppermute(
            lax.slice_in_dim(block, block.shape[dim] - width, None, axis=dim), axis, forward
        )
        high = lax.ppermute(lax.slice_in_dim(block, 0, width, axis=dim), axis, backward)
        block = jnp.concatenate([low, block, high], axis=dim)
    return block


def mask_poles(wide_field):
    lat_index = lax.axis_index("lat")
    lat_count = lax.axis_size("lat")
    total_rows = wide_field.shape[1]
    row_ids = lax.broadcasted_iota(jnp.int32, (1, total_rows, 1, 1), 1)
    upper = jnp.logical_and(row_ids == 0, lat_index == 0)
    lower = jnp.logical_and(row_ids == total_rows - 1, lat_index == lat_count - 1)
    return jnp.where(jnp.logical_or(upper, lower), jnp.zeros((), wide_field.dtype), wide_field)


def pull_product(grad_wide, lat_rows, lon_cols):
    batch_rows = grad_wide.shape[0]
    out_width = grad_wide.shape[3]
    windows = []
    for tap_index in range(9):
        row_off, col_off = divmod(tap_index, 3)
        windows.append(
            grad_wide[
                :, 2 - row_off : 2 - row_off + lat_rows, 2 - col_off : 2 - col_off + lon_cols, :
            ].reshape(-1, out_width)
        )

    def pull_compute(shard_piece, first_row):
        piece_width = shard_piece.shape[0]
        summed = jnp.zeros((batch_rows * lat_rows * lon_cols, piece_width), jnp.float32)
        for tap_index in range(9):
            summed = summed + lax.dot_general(
                windows[tap_index],
                shard_piece[:, tap_index, :],
                (((1,), (1,)), ((), ())),
                preferred_element_type=jnp.float32,
            )
        return summed.reshape(batch_rows, lat_rows, lon_cols, piece_width)

    return pull_compute


def input_taps(act_wide, grad_flat, lat_rows, lon_cols):

    def input_compute(first_row, row_count):
        tap_parts = []
        for tap_index in range(9):
            row_off, col_off = divmod(tap_index, 3)
            tap_slab = act_wide[
                :, row_off : row_off + lat_rows, col_off : col_off + lon_cols, :
            ].reshape(-1, row_count)
            tap_parts.append(
                lax.dot_general(
                    tap_slab,
                    grad_flat,
                    (((0,), (0,)), ((), ())),
                    preferred_element_type=jnp.float32,
                )
            )
        return jnp.stack(tap_parts, axis=1)

    return input_compute


def per_device(activations, upstream, master, moment_one, moment_two):
    lat_rows = activations.shape[1]
    lon_cols = activations.shape[2]
    grad_flat = upstream.reshape(-1, upstream.shape[3])
    act_wide = mask_poles(padded(activations, (("lat", 1), ("lon", 2)), 1))
    grad_wide = mask_poles(padded(upstream, (("lat", 1), ("lon", 2)), 1))
    producer = pull_product(grad_wide, lat_rows, lon_cols)
    term_maker = input_taps(act_wide, grad_flat, lat_rows, lon_cols)
    old_weights = master.astype(jnp.bfloat16)
    old_block = lax.all_gather(old_weights, "lon", axis=0, tiled=True)
    data_sum = producer(lax.all_gather(old_block, "lat", axis=0, tiled=True), jnp.int32(0))
    input_grad = data_sum.astype(jnp.bfloat16)
    shard_rows = master.shape[0]
    lat_block = lax.psum_scatter(
        term_maker(jnp.int32(0), lax.axis_size("lat") * (shard_rows * lax.axis_size("lon"))),
        "lat",
        scatter_dimension=0,
        tiled=True,
    )
    grad_shard = lax.psum_scatter(lat_block, "lon", scatter_dimension=0, tiled=True)
    max_norm = math.sqrt(float(CIN * TAPS * COUT))
    square_sum = lax.psum(jnp.sum(grad_shard * grad_shard), ("lat", "lon"))
    clip_factor = jnp.minimum(1.0, max_norm / (jnp.sqrt(square_sum) + norm_eps))
    grad_scaled = clip_factor * grad_shard
    new_one = beta_one * moment_one + (1.0 - beta_one) * grad_scaled
    new_two = beta_two * moment_two + (1.0 - beta_two) * grad_scaled * grad_scaled
    first_hat = new_one / (1.0 - beta_one**step_count)
    second_hat = new_two / (1.0 - beta_two**step_count)
    new_master = master - learn_rate * (
        first_hat / (jnp.sqrt(second_hat) + adam_eps) + decay_rate * master
    )
    new_half = new_master.astype(jnp.bfloat16)
    lon_block = lax.all_gather(new_half, "lon", axis=0, tiled=True)
    new_weights = lax.all_gather(lon_block, "lat", axis=0, tiled=True)
    return (input_grad, new_weights, new_master, new_one, new_two, grad_scaled)


def solution(mesh):
    in_specs = (
        P(None, "lat", "lon", None),
        P(None, "lat", "lon", None),
        P(("lat", "lon"), None, None),
        P(("lat", "lon"), None, None),
        P(("lat", "lon"), None, None),
    )
    out_specs = (
        P(None, "lat", "lon", None),
        P(),
        P(("lat", "lon"), None, None),
        P(("lat", "lon"), None, None),
        P(("lat", "lon"), None, None),
        P(("lat", "lon"), None, None),
    )
    return jax.shard_map(
        per_device, mesh=mesh, in_specs=in_specs, out_specs=out_specs, check_vma=False
    )
```

profile of v0, /device:TPU:0, one launch (start us, length us, event | category | flops | bytes accessed | tf_op | source)
XLA Modules:
  0.0 431.5 jit_solution(1120258594187733168)
XLA Ops:
  7.2 3.2 fusion.90
  11.2 3.0 collective-permute-start
  20.8 4.6 %collective-permute-done = bf16[4,1,90,512]{3,2,1,0:T(8,128)(2,1)} collective-permute-done((bf16[4,1,90,512]{3,2,1,0:T(8,128)(2,1)}, bf16[4,1,90,512]{3,2,1,0:T(8,128)(2,1)}, u32[]{:S(2)}, u32[]{:S(2)}) %collective-permute-start) | collective-permute-done | bytes 368672 | tf_op jit(solution)/shard_map/ppermute | solution.py:25
  26.8 7.6 %collective-permute-done.1 = bf16[4,1,90,512]{3,2,1,0:T(8,128)(2,1)} collective-permute-done((bf16[4,1,90,512]{3,2,1,0:T(8,128)(2,1)}, bf16[4,1,90,512]{3,2,1,0:T(8,128)(2,1)}, u32[]{:S(2)}, u32[]{:S(2)}) %collective-permute-start.1) | collective-permute-done | bytes 368672 | tf_op jit(solution)/shard_map/ppermute | solution.py:28
  35.6 3.5 collective-permute-start.3
  39.1 3.2 collective-permute-done.4
  43.7 6.5 %collective-permute-done.5 = bf16[4,1,90,512]{3,2,1,0:T(8,128)(2,1)} collective-permute-done((bf16[4,1,90,512]{3,2,1,0:T(8,128)(2,1)S(1)}, bf16[4,1,90,512]{3,2,1,0:T(8,128)(2,1)}, u32[]{:S(2)}, u32[]{:S(2)}) %collective-permute-start.5) | collective-permute-done | bytes 368672 | tf_op jit(solution)/shard_map/ppermute | solution.py:28
  51.3 3.5 collective-permute-start.7
  56.7 2.7 maximum_select_fusion.1
  61.3 2.0 fusion.28
  63.3 2.0 fusion.34
  67.4 2.1 fusion.46
  69.4 2.0 fusion.52
  73.4 2.1 fusion.64
  75.5 2.0 fusion.70
  77.7 95.2 %reduce-scatter.3.cloned.1.call-done = f32[128,9,512]{2,0,1:T(8,128)} async-done(((f32[512,9,512]{2,0,1:T(8,128)}), f32[128,9,512]{2,0,1:T(8,128)}) %reduce-scatter.3.cloned.1.call-update) | async-done | bytes 2359312 | tf_op jit(solution)/shard_map/reduce_scatter | solution.py:105
  173.0 39.4 %reduce-scatter.5.cloned.1.call-done = f32[16,9,512]{2,0,1:T(8,128)} async-done(((f32[128,9,512]{2,0,1:T(8,128)}), f32[16,9,512]{2,0,1:T(8,128)}) %reduce-scatter.5.cloned.1.call-update) | async-done | bytes 294928 | tf_op jit(solution)/shard_map/reduce_scatter | solution.py:111
  214.0 37.9 %psum.7 = f32[]{:T(128)} all-reduce(f32[]{:T(128)} %multiply_reduce_fusion), channel_id=1, replica_groups=mesh['lat'=4,'lon'=8] {'lat','lon'}, use_global_device_ids=true, to_apply=%region_3.4 | all-reduce | flops 1 | bytes 8 | tf_op jit(solution)/shard_map/psum | solution.py:113
  252.6 2.2 fusion.84
  255.4 23.0 %all-gather.5.cloned.1.call-done = bf16[128,9,512]{2,0,1:T(8,128)(2,1)} async-done(((bf16[16,9,512]{2,0,1:T(8,128)(2,1)}), bf16[128,9,512]{2,0,1:T(8,128)(2,1)}) %all-gather.5.cloned.1.call-update) | async-done | bytes 1179664 | tf_op jit(solution)/shard_map/all_gather | solution.py:101
  278.7 24.2 %all-gather.9.cloned.1.call-done = bf16[128,9,512]{2,0,1:T(8,128)(2,1)} async-done(((bf16[16,9,512]{2,0,1:T(8,128)(2,1)}), bf16[128,9,512]{2,0,1:T(8,128)(2,1)}) %all-gather.9.cloned.1.call-update) | async-done | bytes 1179664 | tf_op jit(solution)/shard_map/all_gather | solution.py:124
  302.9 6.2 %fusion.87 = (bf16[4,4,90,512]{3,2,1,0:T(8,128)(2,1)}, bf16[4,4,90,512]{3,2,1,0:T(8,128)(2,1)}, bf16[4,4,90,512]{3,2,1,0:T(8,128)(2,1)}, bf16[4,4,90,512]{3,2,1,...) fusion(bf16[4,6,92,512]{3,2,1,0:T(8,128)(2,1)S(1)} %get-tuple-e, ...), kind=kLoop, calls=%fused_computation.81 | loop fusion | bytes 26542080 | tf_op jit(solution)/shard_map/slice | solution.py:50
  310.9 2.7 reshape.67
  314.9 2.6 reshape.69
  317.5 2.4 reshape.70
  321.2 2.6 reshape.72
  323.8 2.5 reshape.73
  327.6 33.6 %all-gather.7.cloned.1.call-done = bf16[512,9,512]{2,0,1:T(8,128)(2,1)} async-done(((bf16[128,9,512]{2,0,1:T(8,128)(2,1)}), bf16[512,9,512]{2,0,1:T(8,128)(2,1)}) %all-gather.7.cloned.1.call-update) | async-done | bytes 4718608 | tf_op jit(solution)/shard_map/all_gather | solution.py:102
  361.2 2.2 fusion.73
  375.2 2.3 copy.42
  377.4 42.5 %all-gather.11.cloned.1.call-done = bf16[512,9,512]{2,0,1:T(8,128)(2,1)} async-done(((bf16[128,9,512]{2,0,1:T(8,128)(2,1)}), bf16[512,9,512]{2,0,1:T(8,128)(2,1)}) %all-gather.11.cloned.1.call-update) | async-done | bytes 4718608 | tf_op jit(solution)/shard_map/all_gather | solution.py:125
  419.9 4.8 %copy.89 = bf16[512,9,512]{2,0,1:T(8,128)(2,1)} copy(bf16[512,9,512]{2,0,1:T(8,128)(2,1)} %all-gather.11.cloned.1.call-done) | data formatting | bytes 9437184
  (88 shorter events, 40.3 us)
Async XLA Ops:
  7.2 8.8 %copy-start.3 = (bf16[4,4,90,512]{3,1,2,0:T(4,128)(2,1)S(1)}, bf16[4,4,90,512]{3,1,2,0:T(4,128)(2,1)}, u32[]{:S(2)}) copy-start(bf16[4,4,90,512]{3,1,2,0:T(4,128)(2,1)} %param.5) | copy-start | bytes 4423684
  7.2 165.7 %reduce-scatter.3.cloned.1.call-start = ((), (), s32[]{:S(2)}) async-start(), calls=%async_computation.4 | async-start | bytes 11796480 | tf_op jit(solution)/shard_map/reduce_scatter | solution.py:105
  11.2 14.2 %collective-permute-start = (bf16[4,1,90,512]{3,2,1,0:T(8,128)(2,1)}, bf16[4,1,90,512]{3,2,1,0:T(8,128)(2,1)}, u32[]{:S(2)}, u32[]{:S(2)}) collective-permute-start(bf16[4,1,90,512]{3,2,1,0:T(8,128)(2,1)} %copy.72), channel_id=1, source_target_pairs={{0,8},{8,16},{16,24},{24,0},{1,9},{9,17},{17,25},{25,1},{2,10},{10... | collective-permute-start | bytes 1105928 | tf_op jit(solution)/shard_map/ppermute | solution.py:25
  15.0 11.5 %copy-start.4 = (bf16[4,4,90,512]{3,1,2,0:T(4,128)(2,1)S(1)}, bf16[4,4,90,512]{3,1,2,0:T(4,128)(2,1)}, u32[]{:S(2)}) copy-start(bf16[4,4,90,512]{3,1,2,0:T(4,128)(2,1)} %param.6) | copy-start | bytes 4423684
  15.0 19.4 %collective-permute-start.1 = (bf16[4,1,90,512]{3,2,1,0:T(8,128)(2,1)}, bf16[4,1,90,512]{3,2,1,0:T(8,128)(2,1)}, u32[]{:S(2)}, u32[]{:S(2)}) collective-permute-start(bf16[4,1,90,512]{3,2,1,0:T(8,128)(2,1)} %copy.73), channel_id=1, source_target_pairs={{8,0},{16,8},{24,16},{0,24},{9,1},{17,9},{25,17},{1,25},{10,2},{18... | collective-permute-start | bytes 1105928 | tf_op jit(solution)/shard_map/ppermute | solution.py:28
  17.8 24.5 %collective-permute-start.4 = (bf16[4,1,90,512]{3,2,1,0:T(8,128)(2,1)}, bf16[4,1,90,512]{3,2,1,0:T(8,128)(2,1)}, u32[]{:S(2)}, u32[]{:S(2)}) collective-permute-start(bf16[4,1,90,512]{3,2,1,0:T(8,128)(2,1)} %copy.74), channel_id=1, source_target_pairs={{0,8},{8,16},{16,24},{24,0},{1,9},{9,17},{17,25},{25,1},{2,10},{10... | collective-permute-start | bytes 1105928 | tf_op jit(solution)/shard_map/ppermute | solution.py:25
  18.9 31.2 %collective-permute-start.5 = (bf16[4,1,90,512]{3,2,1,0:T(8,128)(2,1)S(1)}, bf16[4,1,90,512]{3,2,1,0:T(8,128)(2,1)}, u32[]{:S(2)}, u32[]{:S(2)}) collective-permute-start(bf16[4,1,90,512]{3,2,1,0:T(8,128)(2,1)S(1)} %copy.75), channel_id=1, source_target_pairs={{8,0},{16,8},{24,16},{0,24},{9,1},{17,9},{25,17},{1,25},{10,2},{18... | collective-permute-start | bytes 1105928 | tf_op jit(solution)/shard_map/ppermute | solution.py:28
  35.5 19.3 %collective-permute-start.2 = (bf16[4,6,1,512]{3,2,1,0:T(2,128)(2,1)S(1)}, bf16[4,6,1,512]{3,2,1,0:T(2,128)(2,1)S(1)}, u32[]{:S(2)}, u32[]{:S(2)}) collective-permute-start(bf16[4,6,1,512]{3,2,1,0:T(2,128)(2,1)S(1)} %get-tuple-element.34), channel_id=1, source_target_pairs={{0,1},{1,2},{2,3},{3,4},{4,5},{5,6},{6,7},{7,0},{8,9},{9,10},{10,1... | collective-permute-start | bytes 73736 | tf_op jit(solution)/shard_map/ppermute | solution.py:25
  35.6 19.3 %collective-permute-start.3 = (bf16[4,6,1,512]{3,2,1,0:T(2,128)(2,1)S(1)}, bf16[4,6,1,512]{3,2,1,0:T(2,128)(2,1)S(1)}, u32[]{:S(2)}, u32[]{:S(2)}) collective-permute-start(bf16[4,6,1,512]{3,2,1,0:T(2,128)(2,1)S(1)} %get-tuple-element.35), channel_id=1, source_target_pairs={{1,0},{2,1},{3,2},{4,3},{5,4},{6,5},{7,6},{0,7},{9,8},{10,9},{11,1... | collective-permute-start | bytes 73736 | tf_op jit(solution)/shard_map/ppermute | solution.py:28
  51.2 5.4 %collective-permute-start.6 = (bf16[4,6,1,512]{3,2,1,0:T(2,128)(2,1)S(1)}, bf16[4,6,1,512]{3,2,1,0:T(2,128)(2,1)S(1)}, u32[]{:S(2)}, u32[]{:S(2)}) collective-permute-start(bf16[4,6,1,512]{3,2,1,0:T(2,128)(2,1)S(1)} %get-tuple-element.23), channel_id=1, source_target_pairs={{0,1},{1,2},{2,3},{3,4},{4,5},{5,6},{6,7},{7,0},{8,9},{9,10},{10,1... | collective-permute-start | bytes 73736 | tf_op jit(solution)/shard_map/ppermute | solution.py:25
  51.3 5.3 %collective-permute-start.7 = (bf16[4,6,1,512]{3,2,1,0:T(2,128)(2,1)S(1)}, bf16[4,6,1,512]{3,2,1,0:T(2,128)(2,1)S(1)}, u32[]{:S(2)}, u32[]{:S(2)}) collective-permute-start(bf16[4,6,1,512]{3,2,1,0:T(2,128)(2,1)S(1)} %get-tuple-element.24), channel_id=1, source_target_pairs={{1,0},{2,1},{3,2},{4,3},{5,4},{6,5},{7,6},{0,7},{9,8},{10,9},{11,1... | collective-permute-start | bytes 73736 | tf_op jit(solution)/shard_map/ppermute | solution.py:28
  54.8 4.5 %copy-start.5 = (bf16[4,4,90,512]{3,1,2,0:T(4,128)(2,1)S(1)}, bf16[4,4,90,512]{3,1,2,0:T(4,128)(2,1)}, u32[]{:S(2)}) copy-start(bf16[4,4,90,512]{3,1,2,0:T(4,128)(2,1)} %param.6) | copy-start | bytes 4423684
  77.6 175.0 %copy-start.15 = (f32[16,9,512]{2,0,1:T(8,128)S(1)}, f32[16,9,512]{2,0,1:T(8,128)}, u32[]{:S(2)}) copy-start(f32[16,9,512]{2,0,1:T(8,128)} %param.7) | copy-start | bytes 884740
  77.6 175.0 %copy-start.16 = (f32[16,9,512]{2,0,1:T(8,128)S(1)}, f32[16,9,512]{2,0,1:T(8,128)}, u32[]{:S(2)}) copy-start(f32[16,9,512]{2,0,1:T(8,128)} %param.8) | copy-start | bytes 884740
  77.6 175.0 %copy-start.17 = (f32[16,9,512]{2,0,1:T(8,128)S(1)}, f32[16,9,512]{2,0,1:T(8,128)}, u32[]{:S(2)}) copy-start(f32[16,9,512]{2,0,1:T(8,128)} %param.9) | copy-start | bytes 884740
  77.6 134.7 %reduce-scatter.5.cloned.1.call-start = ((), (), s32[]{:S(2)}) async-start(), calls=%async_computation.5 | async-start | bytes 2654208 | tf_op jit(solution)/shard_map/reduce_scatter | solution.py:111
  172.9 105.5 %all-gather.5.cloned.1.call-start = ((), (), s32[]{:S(2)}) async-start(), calls=%async_computation.2 | async-start | bytes 1327104 | tf_op jit(solution)/shard_map/all_gather | solution.py:101
  254.8 48.1 %all-gather.9.cloned.1.call-start = ((), (), s32[]{:S(2)}) async-start(), calls=%async_computation.6 | async-start | bytes 1327104 | tf_op jit(solution)/shard_map/all_gather | solution.py:124
  255.4 105.8 %all-gather.7.cloned.1.call-start = ((), (), s32[]{:S(2)}) async-start(), calls=%async_computation.3 | async-start | bytes 5898240 | tf_op jit(solution)/shard_map/all_gather | solution.py:102
  278.4 141.5 %all-gather.11.cloned.1.call-start = ((), (), s32[]{:S(2)}) async-start(), calls=%async_computation.7 | async-start | bytes 5898240 | tf_op jit(solution)/shard_map/all_gather | solution.py:125
  309.1 4.4 %copy-start.2 = (bf16[4,4,90,512]{3,2,1,0:T(8,128)(2,1)S(1)}, bf16[4,4,90,512]{3,2,1,0:T(8,128)(2,1)}, u32[]{:S(2)}) copy-start(bf16[4,4,90,512]{3,2,1,0:T(8,128)(2,1)} %get-tuple-element.31) | copy-start | bytes 4423684
  314.9 5.0 %copy-start.1 = (bf16[4,4,90,512]{3,2,1,0:T(8,128)(2,1)S(1)}, bf16[4,4,90,512]{3,2,1,0:T(8,128)(2,1)}, u32[]{:S(2)}) copy-start(bf16[4,4,90,512]{3,2,1,0:T(8,128)(2,1)} %get-tuple-element.28) | copy-start | bytes 4423684
  321.2 5.1 %copy-start = (bf16[4,4,90,512]{3,2,1,0:T(8,128)(2,1)S(1)}, bf16[4,4,90,512]{3,2,1,0:T(8,128)(2,1)}, u32[]{:S(2)}) copy-start(bf16[4,4,90,512]{3,2,1,0:T(8,128)(2,1)} %get-tuple-element.25) | copy-start | bytes 4423684
  327.6 35.8 %copy-start.13 = (bf16[1440,512]{1,0:T(8,128)(2,1)S(1)}, bf16[1440,512]{1,0:T(8,128)(2,1)}, u32[]{:S(2)}) copy-start(bf16[1440,512]{1,0:T(8,128)(2,1)} %reshape.67) | copy-start | bytes 4423684
  361.2 2.5 copy-start.14
  363.7 1.4 copy-start.12
  365.1 1.4 copy-start.11
  366.5 1.4 copy-start.10
  367.8 1.4 copy-start.9
  369.2 1.6 copy-start.8
  370.8 1.5 copy-start.7
  372.3 1.5 copy-start.6
Sparse Core Ops, SparseCore 0:
  77.7 95.1 reduce-scatter.2
  175.2 37.0 reduce-scatter.4
  254.9 23.4 all-gather.4
  280.4 22.4 all-gather.8
  304.6 56.5 all-gather.6
  362.9 56.9 all-gather.10
where the time goes:
time: 432 us
  waiting for transfers between devices  282 us (65%)
  local copies, waits for them, and re-layouts  47.3 us (11%)
  blocking collectives  37.9 us (9%)
  matrix products  28.2 us (7%)
  between operations  15.1 us (3%)
  starting transfers between devices  14.5 us (3%)
  other arithmetic  6.48 us (2%)
    reduce_scatter x1, waiting for transfers between devices, per_device(): lax.psum_scatter(term_maker(jnp.int32(0), lax.axis_size('lat') * (shard_r...  95.2 us
    all_gather x1, waiting for transfers between devices, per_device(): new_weights = lax.all_gather(lon_block, 'lat', axis=0, tiled=True)  42.5 us
    reduce_scatter x1, waiting for transfers between devices, per_device(): lax.psum_scatter(lat_block, 'lon', scatter_dimension=0, tiled=True)  39.4 us
    psum x1, blocking collectives, per_device(): square_sum = lax.psum(jnp.sum(grad_shard * grad_shard), ('lat', 'lon'))  37.9 us
    all_gather x1, waiting for transfers between devices, per_device(): lax.all_gather(old_block, 'lat', axis=0, tiled=True)  33.6 us
    all_gather x1, waiting for transfers between devices, per_device(): lon_block = lax.all_gather(new_half, 'lon', axis=0, tiled=True)  24.2 us
    all_gather x1, waiting for transfers between devices, per_device(): old_block = lax.all_gather(old_weights, 'lon', axis=0, tiled=True)  23 us
    reshape x9, local copies, waits for them, and re-layouts, pull_product(): windows.append(grad_wide[:, 2 - row_off:2 - row_off + lat_rows, 2 - col_o...  18.5 us
  transfers between devices with their start and end apart: 14, of which 11 were waited for; matrix products, arithmetic and copies ran while one was open for 10% of the time, Pallas kernels for 0%

commit v1 on v0

--- a/solution.py
+++ b/solution.py
@@ -121,7 +121,12 @@
         first_hat / (jnp.sqrt(second_hat) + adam_eps) + decay_rate * master
     )
     new_half = new_master.astype(jnp.bfloat16)
-    lon_block = lax.all_gather(new_half, "lon", axis=0, tiled=True)
+    ring = [new_half]
+    for hop in range(7):
+        ring.append(lax.ppermute(ring[-1], "lon", [(dev, (dev + 1) % 8) for dev in range(8)]))
+    lon_block = jnp.roll(
+        jnp.concatenate(ring[::-1], axis=0), (lax.axis_index("lon") + 1) * ring[0].shape[0], axis=0
+    )
     new_weights = lax.all_gather(lon_block, "lat", axis=0, tiled=True)
     return (input_grad, new_weights, new_master, new_one, new_two, grad_scaled)
 

time: 432 us -> 468 us (1.083)
  waiting for transfers between devices: 282 us -> 321 us
    ppermute x0 -> x7, waiting for transfers between devices: none -> 44.2 us  [per_device(): lax.ppermute(ring[-1], 'lon', [(dev, (dev + 1) % 8) for dev in range(8)])]
    all_gather x1, waiting for transfers between devices: 33.6 us -> 58.7 us  [per_device(): lax.all_gather(old_block, 'lat', axis=0, tiled=True)]
    all_gather x1 -> x0, waiting for transfers between devices: 24.2 us -> none  [per_device(): lon_block = lax.all_gather(new_half, 'lon', axis=0, tiled=True)]
    ppermute x4, waiting for transfers between devices: 14.1 us -> 23.3 us  [padded(): lax.ppermute(lax.slice_in_dim(block, 0, width, axis=dim), axis, backward)]
    all_gather x1, waiting for transfers between devices: 23 us -> 16.4 us  [per_device(): old_block = lax.all_gather(old_weights, 'lon', axis=0, tiled=True)]
    all_gather x1, waiting for transfers between devices: 42.5 us -> 36.1 us  [per_device(): new_weights = lax.all_gather(lon_block, 'lat', axis=0, tiled=True)]
    unnamed x46 -> x65, local copies, waits for them, and re-layouts: 15.8 us -> 15.6 us
  transfers between devices with their start and end apart: 14 -> 20, of which waited for: 11 -> 15; matrix products, arithmetic and copies ran while one was open for 10% -> 7% of each run, Pallas kernels for 0% -> 0%
where the time goes in v1:
time: 468 us; the launch traced here: 467 us
  waiting for transfers between devices  321 us (69%)
  local copies, waits for them, and re-layouts  45.7 us (10%)
  blocking collectives  38 us (8%)
  matrix products  28.1 us (6%)
  between operations  15 us (3%)
  starting transfers between devices  13.6 us (3%)
  other arithmetic  6.43 us (1%)
    reduce_scatter x1, waiting for transfers between devices, per_device(): lax.psum_scatter(term_maker(jnp.int32(0), lax.axis_size('lat') * (shard_r...  95 us
    all_gather x1, waiting for transfers between devices, per_device(): lax.all_gather(old_block, 'lat', axis=0, tiled=True)  58.7 us
    ppermute x7, waiting for transfers between devices, per_device(): lax.ppermute(ring[-1], 'lon', [(dev, (dev + 1) % 8) for dev in range(8)])  44.2 us
    reduce_scatter x1, waiting for transfers between devices, per_device(): lax.psum_scatter(lat_block, 'lon', scatter_dimension=0, tiled=True)  39.3 us
    psum x1, blocking collectives, per_device(): square_sum = lax.psum(jnp.sum(grad_shard * grad_shard), ('lat', 'lon'))  38 us
    all_gather x1, waiting for transfers between devices, per_device(): new_weights = lax.all_gather(lon_block, 'lat', axis=0, tiled=True)  36.1 us
    ppermute x4, waiting for transfers between devices, padded(): lax.ppermute(lax.slice_in_dim(block, 0, width, axis=dim), axis, backward)  23.3 us
    dot_general x9, matrix products, input_compute(): lax.dot_general(tap_slab, grad_flat, (((0,), (0,)), ((), ())), preferred_...  18.2 us
  transfers between devices with their start and end apart: 20, of which 15 were waited for; matrix products, arithmetic and copies ran while one was open for 7% of the time, Pallas kernels for 0%

profile of v1, /device:TPU:0, one launch (start us, length us, event | category | flops | bytes accessed | tf_op | source)
XLA Modules:
  0.0 467.4 jit_solution(14868597112934487830)
XLA Ops:
  7.2 3.2 fusion.90
  11.2 3.0 collective-permute-start
  20.0 5.5 %collective-permute-done = bf16[4,1,90,512]{3,2,1,0:T(8,128)(2,1)} collective-permute-done((bf16[4,1,90,512]{3,2,1,0:T(8,128)(2,1)}, bf16[4,1,90,512]{3,2,1,0:T(8,128)(2,1)}, u32[]{:S(2)}, u32[]{:S(2)}) %collective-permute-start) | collective-permute-done | bytes 368672 | tf_op jit(solution)/shard_map/ppermute | solution.py:25
  26.8 23.3 %collective-permute-done.1 = bf16[4,1,90,512]{3,2,1,0:T(8,128)(2,1)} collective-permute-done((bf16[4,1,90,512]{3,2,1,0:T(8,128)(2,1)}, bf16[4,1,90,512]{3,2,1,0:T(8,128)(2,1)}, u32[]{:S(2)}, u32[]{:S(2)}) %collective-permute-start.1) | collective-permute-done | bytes 368672 | tf_op jit(solution)/shard_map/ppermute | solution.py:28
  51.3 3.5 collective-permute-start.3
  57.4 3.5 collective-permute-start.7
  62.9 2.7 maximum_select_fusion.1
  73.6 2.0 fusion.46
  75.7 2.0 fusion.52
  79.7 2.1 fusion.64
  83.9 95.0 %reduce-scatter.3.cloned.1.call-done = f32[128,9,512]{2,0,1:T(8,128)} async-done(((f32[512,9,512]{2,0,1:T(8,128)}), f32[128,9,512]{2,0,1:T(8,128)}) %reduce-scatter.3.cloned.1.call-update) | async-done | bytes 2359312 | tf_op jit(solution)/shard_map/reduce_scatter | solution.py:105
  179.0 39.3 %reduce-scatter.5.cloned.1.call-done = f32[16,9,512]{2,0,1:T(8,128)} async-done(((f32[128,9,512]{2,0,1:T(8,128)}), f32[16,9,512]{2,0,1:T(8,128)}) %reduce-scatter.5.cloned.1.call-update) | async-done | bytes 294928 | tf_op jit(solution)/shard_map/reduce_scatter | solution.py:111
  219.9 38.0 %psum.7 = f32[]{:T(128)} all-reduce(f32[]{:T(128)} %multiply_reduce_fusion), channel_id=1, replica_groups=mesh['lat'=4,'lon'=8] {'lat','lon'}, use_global_device_ids=true, to_apply=%region_3.4 | all-reduce | flops 1 | bytes 8 | tf_op jit(solution)/shard_map/psum | solution.py:113
  258.7 2.1 fusion.84
  260.8 6.4 %collective-permute-done.8 = bf16[16,9,512]{2,0,1:T(8,128)(2,1)S(1)} collective-permute-done((bf16[16,9,512]{2,0,1:T(8,128)(2,1)S(1)}, bf16[16,9,512]{2,0,1:T(8,128)(2,1)S(1)}, u32[]{:S(2)}, u32[]{:S(2)}) %collective-permute-start.8) | collective-permute-done | bytes 147488 | tf_op jit(solution)/shard_map/ppermute | solution.py:126
  267.2 6.4 %collective-permute-done.9 = bf16[16,9,512]{2,0,1:T(8,128)(2,1)S(1)} collective-permute-done((bf16[16,9,512]{2,0,1:T(8,128)(2,1)S(1)}, bf16[16,9,512]{2,0,1:T(8,128)(2,1)S(1)}, u32[]{:S(2)}, u32[]{:S(2)}) %collective-permute-start.9) | collective-permute-done | bytes 147488 | tf_op jit(solution)/shard_map/ppermute | solution.py:126
  273.5 6.4 %collective-permute-done.10 = bf16[16,9,512]{2,0,1:T(8,128)(2,1)S(1)} collective-permute-done((bf16[16,9,512]{2,0,1:T(8,128)(2,1)S(1)}, bf16[16,9,512]{2,0,1:T(8,128)(2,1)S(1)}, u32[]{:S(2)}, u32[]{:S(2)}) %collective-permute-start.10) | collective-permute-done | bytes 147488 | tf_op jit(solution)/shard_map/ppermute | solution.py:126
  279.9 6.4 %collective-permute-done.11 = bf16[16,9,512]{2,0,1:T(8,128)(2,1)S(1)} collective-permute-done((bf16[16,9,512]{2,0,1:T(8,128)(2,1)S(1)}, bf16[16,9,512]{2,0,1:T(8,128)(2,1)S(1)}, u32[]{:S(2)}, u32[]{:S(2)}) %collective-permute-start.11) | collective-permute-done | bytes 147488 | tf_op jit(solution)/shard_map/ppermute | solution.py:126
  286.3 6.4 %collective-permute-done.12 = bf16[16,9,512]{2,0,1:T(8,128)(2,1)S(1)} collective-permute-done((bf16[16,9,512]{2,0,1:T(8,128)(2,1)S(1)}, bf16[16,9,512]{2,0,1:T(8,128)(2,1)S(1)}, u32[]{:S(2)}, u32[]{:S(2)}) %collective-permute-start.12) | collective-permute-done | bytes 147488 | tf_op jit(solution)/shard_map/ppermute | solution.py:126
  292.6 6.4 %collective-permute-done.13 = bf16[16,9,512]{2,0,1:T(8,128)(2,1)S(1)} collective-permute-done((bf16[16,9,512]{2,0,1:T(8,128)(2,1)S(1)}, bf16[16,9,512]{2,0,1:T(8,128)(2,1)S(1)}, u32[]{:S(2)}, u32[]{:S(2)}) %collective-permute-start.13) | collective-permute-done | bytes 147488 | tf_op jit(solution)/shard_map/ppermute | solution.py:126
  299.3 6.0 %collective-permute-done.14 = bf16[16,9,512]{2,0,1:T(8,128)(2,1)S(1)} collective-permute-done((bf16[16,9,512]{2,0,1:T(8,128)(2,1)S(1)}, bf16[16,9,512]{2,0,1:T(8,128)(2,1)S(1)}, u32[]{:S(2)}, u32[]{:S(2)}) %collective-permute-start.14) | collective-permute-done | bytes 147488 | tf_op jit(solution)/shard_map/ppermute | solution.py:126
  306.8 16.4 %all-gather.4.cloned.1.call-done = bf16[128,9,512]{2,0,1:T(8,128)(2,1)} async-done(((bf16[16,9,512]{2,0,1:T(8,128)(2,1)}), bf16[128,9,512]{2,0,1:T(8,128)(2,1)}) %all-gather.4.cloned.1.call-update) | async-done | bytes 1179664 | tf_op jit(solution)/shard_map/all_gather | solution.py:101
  323.3 6.2 %fusion.87 = (bf16[4,4,90,512]{3,2,1,0:T(8,128)(2,1)}, bf16[4,4,90,512]{3,2,1,0:T(8,128)(2,1)}, bf16[4,4,90,512]{3,2,1,0:T(8,128)(2,1)}, bf16[4,4,90,512]{3,2,1,...) fusion(bf16[4,6,92,512]{3,2,1,0:T(8,128)(2,1)S(1)} %get-tuple-e, ...), kind=kLoop, calls=%fused_computation.98 | loop fusion | bytes 26542080 | tf_op jit(solution)/shard_map/slice | solution.py:50
  329.5 2.6 reshape.74
  334.8 2.7 reshape.71
  340.1 2.6 reshape.68
  342.6 2.4 reshape.67
  345.5 36.1 %all-gather.8.cloned.1.call-done = bf16[512,9,512]{2,0,1:T(8,128)(2,1)} async-done(((bf16[128,9,512]{2,0,1:T(8,128)(2,1)}), bf16[512,9,512]{2,0,1:T(8,128)(2,1)}) %all-gather.8.cloned.1.call-update) | async-done | bytes 4718608 | tf_op jit(solution)/shard_map/all_gather | solution.py:130
  381.6 58.7 %all-gather.6.cloned.1.call-done = bf16[512,9,512]{2,0,1:T(8,128)(2,1)} async-done(((bf16[128,9,512]{2,0,1:T(8,128)(2,1)}), bf16[512,9,512]{2,0,1:T(8,128)(2,1)}) %all-gather.6.cloned.1.call-update) | async-done | bytes 4718608 | tf_op jit(solution)/shard_map/all_gather | solution.py:102
  440.2 2.2 fusion.73
  453.8 2.3 copy.42
  456.0 4.8 %copy.104 = bf16[512,9,512]{2,0,1:T(8,128)(2,1)} copy(bf16[512,9,512]{2,0,1:T(8,128)(2,1)} %all-gather.8.cloned.1.call-done) | data formatting | bytes 9437184
  (120 shorter events, 46.1 us)
Async XLA Ops:
  7.2 7.0 %copy-start.5 = (bf16[4,4,90,512]{3,1,2,0:T(4,128)(2,1)S(1)}, bf16[4,4,90,512]{3,1,2,0:T(4,128)(2,1)}, u32[]{:S(2)}) copy-start(bf16[4,4,90,512]{3,1,2,0:T(4,128)(2,1)} %param.5) | copy-start | bytes 4423684
  7.2 171.8 %reduce-scatter.3.cloned.1.call-start = ((), (), s32[]{:S(2)}) async-start(), calls=%async_computation.4 | async-start | bytes 11796480 | tf_op jit(solution)/shard_map/reduce_scatter | solution.py:105
  11.2 14.2 %collective-permute-start = (bf16[4,1,90,512]{3,2,1,0:T(8,128)(2,1)}, bf16[4,1,90,512]{3,2,1,0:T(8,128)(2,1)}, u32[]{:S(2)}, u32[]{:S(2)}) collective-permute-start(bf16[4,1,90,512]{3,2,1,0:T(8,128)(2,1)} %copy.72), channel_id=1, source_target_pairs={{0,8},{8,16},{16,24},{24,0},{1,9},{9,17},{17,25},{25,1},{2,10},{10... | collective-permute-start | bytes 1105928 | tf_op jit(solution)/shard_map/ppermute | solution.py:25
  15.2 11.2 %copy-start.6 = (bf16[4,4,90,512]{3,1,2,0:T(4,128)(2,1)S(1)}, bf16[4,4,90,512]{3,1,2,0:T(4,128)(2,1)}, u32[]{:S(2)}) copy-start(bf16[4,4,90,512]{3,1,2,0:T(4,128)(2,1)} %param.6) | copy-start | bytes 4423684
  16.1 38.8 %collective-permute-start.4 = (bf16[4,1,90,512]{3,2,1,0:T(8,128)(2,1)}, bf16[4,1,90,512]{3,2,1,0:T(8,128)(2,1)}, u32[]{:S(2)}, u32[]{:S(2)}) collective-permute-start(bf16[4,1,90,512]{3,2,1,0:T(8,128)(2,1)} %copy.74), channel_id=1, source_target_pairs={{0,8},{8,16},{16,24},{24,0},{1,9},{9,17},{17,25},{25,1},{2,10},{10... | collective-permute-start | bytes 1105928 | tf_op jit(solution)/shard_map/ppermute | solution.py:25
  17.6 38.6 %collective-permute-start.5 = (bf16[4,1,90,512]{3,2,1,0:T(8,128)(2,1)S(1)}, bf16[4,1,90,512]{3,2,1,0:T(8,128)(2,1)}, u32[]{:S(2)}, u32[]{:S(2)}) collective-permute-start(bf16[4,1,90,512]{3,2,1,0:T(8,128)(2,1)S(1)} %copy.75), channel_id=1, source_target_pairs={{8,0},{16,8},{24,16},{0,24},{9,1},{17,9},{25,17},{1,25},{10,2},{18... | collective-permute-start | bytes 1105928 | tf_op jit(solution)/shard_map/ppermute | solution.py:28
  19.9 30.2 %collective-permute-start.1 = (bf16[4,1,90,512]{3,2,1,0:T(8,128)(2,1)}, bf16[4,1,90,512]{3,2,1,0:T(8,128)(2,1)}, u32[]{:S(2)}, u32[]{:S(2)}) collective-permute-start(bf16[4,1,90,512]{3,2,1,0:T(8,128)(2,1)} %copy.73), channel_id=1, source_target_pairs={{8,0},{16,8},{24,16},{0,24},{9,1},{17,9},{25,17},{1,25},{10,2},{18... | collective-permute-start | bytes 1105928 | tf_op jit(solution)/shard_map/ppermute | solution.py:28
  51.2 9.7 %collective-permute-start.2 = (bf16[4,6,1,512]{3,2,1,0:T(2,128)(2,1)S(1)}, bf16[4,6,1,512]{3,2,1,0:T(2,128)(2,1)S(1)}, u32[]{:S(2)}, u32[]{:S(2)}) collective-permute-start(bf16[4,6,1,512]{3,2,1,0:T(2,128)(2,1)S(1)} %get-tuple-element.34), channel_id=1, source_target_pairs={{0,1},{1,2},{2,3},{3,4},{4,5},{5,6},{6,7},{7,0},{8,9},{9,10},{10,1... | collective-permute-start | bytes 73736 | tf_op jit(solution)/shard_map/ppermute | solution.py:25
  51.3 9.6 %collective-permute-start.3 = (bf16[4,6,1,512]{3,2,1,0:T(2,128)(2,1)S(1)}, bf16[4,6,1,512]{3,2,1,0:T(2,128)(2,1)S(1)}, u32[]{:S(2)}, u32[]{:S(2)}) collective-permute-start(bf16[4,6,1,512]{3,2,1,0:T(2,128)(2,1)S(1)} %get-tuple-element.35), channel_id=1, source_target_pairs={{1,0},{2,1},{3,2},{4,3},{5,4},{6,5},{7,6},{0,7},{9,8},{10,9},{11,1... | collective-permute-start | bytes 73736 | tf_op jit(solution)/shard_map/ppermute | solution.py:28
  57.3 5.6 %collective-permute-start.6 = (bf16[4,6,1,512]{3,2,1,0:T(2,128)(2,1)S(1)}, bf16[4,6,1,512]{3,2,1,0:T(2,128)(2,1)S(1)}, u32[]{:S(2)}, u32[]{:S(2)}) collective-permute-start(bf16[4,6,1,512]{3,2,1,0:T(2,128)(2,1)S(1)} %get-tuple-element.23), channel_id=1, source_target_pairs={{0,1},{1,2},{2,3},{3,4},{4,5},{5,6},{6,7},{7,0},{8,9},{9,10},{10,1... | collective-permute-start | bytes 73736 | tf_op jit(solution)/shard_map/ppermute | solution.py:25
  57.4 5.5 %collective-permute-start.7 = (bf16[4,6,1,512]{3,2,1,0:T(2,128)(2,1)S(1)}, bf16[4,6,1,512]{3,2,1,0:T(2,128)(2,1)S(1)}, u32[]{:S(2)}, u32[]{:S(2)}) collective-permute-start(bf16[4,6,1,512]{3,2,1,0:T(2,128)(2,1)S(1)} %get-tuple-element.24), channel_id=1, source_target_pairs={{1,0},{2,1},{3,2},{4,3},{5,4},{6,5},{7,6},{0,7},{9,8},{10,9},{11,1... | collective-permute-start | bytes 73736 | tf_op jit(solution)/shard_map/ppermute | solution.py:28
  60.9 4.7 copy-start.7
  83.8 174.8 %copy-start.17 = (f32[16,9,512]{2,0,1:T(8,128)S(1)}, f32[16,9,512]{2,0,1:T(8,128)}, u32[]{:S(2)}) copy-start(f32[16,9,512]{2,0,1:T(8,128)} %param.7) | copy-start | bytes 884740
  83.8 174.8 %copy-start.18 = (f32[16,9,512]{2,0,1:T(8,128)S(1)}, f32[16,9,512]{2,0,1:T(8,128)}, u32[]{:S(2)}) copy-start(f32[16,9,512]{2,0,1:T(8,128)} %param.8) | copy-start | bytes 884740
  83.8 174.8 %copy-start.19 = (f32[16,9,512]{2,0,1:T(8,128)S(1)}, f32[16,9,512]{2,0,1:T(8,128)}, u32[]{:S(2)}) copy-start(f32[16,9,512]{2,0,1:T(8,128)} %param.9) | copy-start | bytes 884740
  83.9 134.4 %reduce-scatter.5.cloned.1.call-start = ((), (), s32[]{:S(2)}) async-start(), calls=%async_computation.5 | async-start | bytes 2654208 | tf_op jit(solution)/shard_map/reduce_scatter | solution.py:111
  179.0 144.3 %all-gather.4.cloned.1.call-start = ((), (), s32[]{:S(2)}) async-start(), calls=%async_computation.2 | async-start | bytes 1327104 | tf_op jit(solution)/shard_map/all_gather | solution.py:101
  260.8 6.4 %collective-permute-start.8 = (bf16[16,9,512]{2,0,1:T(8,128)(2,1)S(1)}, bf16[16,9,512]{2,0,1:T(8,128)(2,1)S(1)}, u32[]{:S(2)}, u32[]{:S(2)}) collective-permute-start(bf16[16,9,512]{2,0,1:T(8,128)(2,1)S(1)} %get-tuple-element.18), channel_id=1, source_target_pairs={{0,1},{1,2},{2,3},{3,4},{4,5},{5,6},{6,7},{7,0},{8,9},{9,10},{10,1... | collective-permute-start | bytes 442376 | tf_op jit(solution)/shard_map/ppermute | solution.py:126
  267.1 6.4 %collective-permute-start.9 = (bf16[16,9,512]{2,0,1:T(8,128)(2,1)S(1)}, bf16[16,9,512]{2,0,1:T(8,128)(2,1)S(1)}, u32[]{:S(2)}, u32[]{:S(2)}) collective-permute-start(bf16[16,9,512]{2,0,1:T(8,128)(2,1)S(1)} %collective-permute-done.8), channel_id=1, source_target_pairs={{0,1},{1,2},{2,3},{3,4},{4,5},{5,6},{6,7},{7,0},{8,9},{9,10},{10,1... | collective-permute-start | bytes 442376 | tf_op jit(solution)/shard_map/ppermute | solution.py:126
  273.5 6.4 %collective-permute-start.10 = (bf16[16,9,512]{2,0,1:T(8,128)(2,1)S(1)}, bf16[16,9,512]{2,0,1:T(8,128)(2,1)S(1)}, u32[]{:S(2)}, u32[]{:S(2)}) collective-permute-start(bf16[16,9,512]{2,0,1:T(8,128)(2,1)S(1)} %collective-permute-done.9), channel_id=1, source_target_pairs={{0,1},{1,2},{2,3},{3,4},{4,5},{5,6},{6,7},{7,0},{8,9},{9,10},{10,1... | collective-permute-start | bytes 442376 | tf_op jit(solution)/shard_map/ppermute | solution.py:126
  279.9 6.4 %collective-permute-start.11 = (bf16[16,9,512]{2,0,1:T(8,128)(2,1)S(1)}, bf16[16,9,512]{2,0,1:T(8,128)(2,1)S(1)}, u32[]{:S(2)}, u32[]{:S(2)}) collective-permute-start(bf16[16,9,512]{2,0,1:T(8,128)(2,1)S(1)} %collective-permute-done.10), channel_id=1, source_target_pairs={{0,1},{1,2},{2,3},{3,4},{4,5},{5,6},{6,7},{7,0},{8,9},{9,10},{10,1... | collective-permute-start | bytes 442376 | tf_op jit(solution)/shard_map/ppermute | solution.py:126
  286.2 6.4 %collective-permute-start.12 = (bf16[16,9,512]{2,0,1:T(8,128)(2,1)S(1)}, bf16[16,9,512]{2,0,1:T(8,128)(2,1)S(1)}, u32[]{:S(2)}, u32[]{:S(2)}) collective-permute-start(bf16[16,9,512]{2,0,1:T(8,128)(2,1)S(1)} %collective-permute-done.11), channel_id=1, source_target_pairs={{0,1},{1,2},{2,3},{3,4},{4,5},{5,6},{6,7},{7,0},{8,9},{9,10},{10,1... | collective-permute-start | bytes 442376 | tf_op jit(solution)/shard_map/ppermute | solution.py:126
  292.6 6.4 %collective-permute-start.13 = (bf16[16,9,512]{2,0,1:T(8,128)(2,1)S(1)}, bf16[16,9,512]{2,0,1:T(8,128)(2,1)S(1)}, u32[]{:S(2)}, u32[]{:S(2)}) collective-permute-start(bf16[16,9,512]{2,0,1:T(8,128)(2,1)S(1)} %collective-permute-done.12), channel_id=1, source_target_pairs={{0,1},{1,2},{2,3},{3,4},{4,5},{5,6},{6,7},{7,0},{8,9},{9,10},{10,1... | collective-permute-start | bytes 442376 | tf_op jit(solution)/shard_map/ppermute | solution.py:126
  299.0 6.4 %collective-permute-start.14 = (bf16[16,9,512]{2,0,1:T(8,128)(2,1)S(1)}, bf16[16,9,512]{2,0,1:T(8,128)(2,1)S(1)}, u32[]{:S(2)}, u32[]{:S(2)}) collective-permute-start(bf16[16,9,512]{2,0,1:T(8,128)(2,1)S(1)} %collective-permute-done.13), channel_id=1, source_target_pairs={{0,1},{1,2},{2,3},{3,4},{4,5},{5,6},{6,7},{7,0},{8,9},{9,10},{10,1... | collective-permute-start | bytes 442376 | tf_op jit(solution)/shard_map/ppermute | solution.py:126
  299.0 82.5 %all-gather.8.cloned.1.call-start = ((), (), s32[]{:S(2)}) async-start(), calls=%async_computation.6 | async-start | bytes 5898240 | tf_op jit(solution)/shard_map/all_gather | solution.py:130
  306.8 133.4 %all-gather.6.cloned.1.call-start = ((), (), s32[]{:S(2)}) async-start(), calls=%async_computation.3 | async-start | bytes 5898240 | tf_op jit(solution)/shard_map/all_gather | solution.py:102
  329.5 2.6 copy-start.4
  329.5 4.0 copy-start.3
  333.4 4.0 copy-start.2
  334.8 4.0 copy-start.1
  340.1 5.0 %copy-start = (bf16[4,4,90,512]{3,2,1,0:T(8,128)(2,1)S(1)}, bf16[4,4,90,512]{3,2,1,0:T(8,128)(2,1)}, u32[]{:S(2)}) copy-start(bf16[4,4,90,512]{3,2,1,0:T(8,128)(2,1)} %get-tuple-element.33) | copy-start | bytes 4423684
  345.5 96.9 %copy-start.15 = (bf16[1440,512]{1,0:T(8,128)(2,1)S(1)}, bf16[1440,512]{1,0:T(8,128)(2,1)}, u32[]{:S(2)}) copy-start(bf16[1440,512]{1,0:T(8,128)(2,1)} %reshape.67) | copy-start | bytes 4423684
  (8 other events, 12.1 us)
Sparse Core Ops, SparseCore 0:
  83.9 94.9 reduce-scatter.2
  181.3 36.9 reduce-scatter.4
  299.1 24.0 all-gather.3
  324.9 56.5 all-gather.7
  383.3 56.9 all-gather.5
